TPU v7x, 32 devices: a whole 2x2x4 slice. The times are simulated.
32 devices in a mesh: seq: 4 (over y, x), tp: 8 (over z, core).
Axes of the slice: x: 2, y: 2, z: 4, core: 2. Of those that a mesh axis runs over, the one named last changes fastest.
Arguments:
- tokens: bfloat16 [1024, 4096], P('seq', 'tp'), may hold values from -30 to 30
- w_qkv: bfloat16 [4096, 3, 2048], P('seq', None, 'tp'), may hold values from -1 to 1
- keep_list: int32 [512], P('seq'), may hold values from 0 to 255, as said below
- counts: int32 [4], P('seq'), may hold values from 1 to 127, as said below
Outputs:
- attended: bfloat16 [256, 2048], P('seq', 'tp')
Inputs may be any that keep to these rules, and one draw needn't show every extreme that they name: `counts`: the entries sum to 256; one shard keeps 2 * 64 - 1 tokens and one shard keeps 1. `keep_list`: entries s * 2 * 64 to s * 2 * 64 + 2 * 64 - 1 are distinct token indices within shard s; the first counts[s] of them increase.
All inputs are finite; a program needn't handle non-finite values.
Results may differ from a plain program's by a relative error of at most 0.0065.
Values may be sent and summed in bfloat16 or wider, within the bound.
No kernel may reach another device: no remote copies, remote signals or barrier semaphores. Data moves between devices by JAX's collectives and lax.ppermute only.
A program may use at most 64 MiB of HBM per device.

v0:
```python
import jax
import jax.numpy as jnp
from jax import lax
from jax.sharding import PartitionSpec as P

HD = 128


def entering(value, axis, join, neutral):
    count, mine = (lax.axis_size(axis), lax.axis_index(axis))
    pieces = lax.all_gather(value, axis)
    so_far = jnp.full_like(value, 0) + jnp.asarray(neutral, value.dtype)

    def lap(position, so_far):
        longer = join(so_far, pieces[position])
        return jnp.where(position < mine, longer, so_far)

    return lax.fori_loop(0, count - 1, lap, so_far)


def add_sums(earlier, later):
    return earlier + later


def on_device(tokens, w_qkv, keep_list, counts):
    shards = lax.axis_size("seq")
    my_index = lax.axis_index("seq")
    tok_dev = tokens.shape[0]
    slots = keep_list.shape[0]
    capacity = slots // 2
    per_peer = slots // shards
    head_dim = HD
    columns = w_qkv.shape[2]
    local_heads = columns // head_dim
    offset = entering(counts, "seq", add_sums, jnp.zeros_like(counts))[0]
    peers = jnp.arange(shards, dtype=jnp.int32)[:, None]
    rounds = jnp.arange(per_peer, dtype=jnp.int32)[None, :]
    local_slot = (peers - offset) % shards + rounds * shards
    live = local_slot < counts[0]
    token_index = keep_list[local_slot]
    ranks = jnp.where(live, offset + local_slot, -1).astype(jnp.int32)
    positions = my_index * tok_dev + token_index
    meta = jnp.stack([positions, ranks], axis=2)
    picked = jnp.where(live[:, :, None], tokens[token_index], jnp.zeros((), tokens.dtype))
    arrived, arrived_meta = (
        lax.all_to_all(picked, "seq", split_axis=0, concat_axis=0, tiled=True),
        lax.all_to_all(meta, "seq", split_axis=0, concat_axis=0, tiled=True),
    )
    arrived_meta = arrived_meta.reshape(shards * per_peer, 2)
    arrived_rank = arrived_meta[:, 1]
    target = jnp.where(arrived_rank >= 0, arrived_rank // shards, capacity)
    flat = arrived.reshape(shards * per_peer, arrived.shape[2])
    kept = jnp.zeros((capacity, flat.shape[1]), flat.dtype).at[target].set(flat, mode="drop")
    kept_pos = jnp.zeros((capacity,), jnp.int32).at[target].set(arrived_meta[:, 0], mode="drop")
    full_rows = lax.all_gather(kept, "tp", axis=1, tiled=True)
    piece = lax.all_gather(w_qkv, "seq", axis=0, tiled=True)
    part_rows = lax.slice_in_dim(full_rows, 0, piece.shape[0], axis=1)
    projected = jnp.einsum(
        "rd,dgc->rgc", part_rows, piece, preferred_element_type=jnp.float32
    ).astype(jnp.bfloat16)
    queries = projected[:, 0].reshape(capacity, local_heads, head_dim)
    key_values = projected[:, 1:]
    scale = head_dim ** (-0.5)
    all_kv, all_pos = (
        lax.all_gather(key_values, "seq", axis=0, tiled=True),
        lax.all_gather(kept_pos, "seq", axis=0, tiled=True),
    )
    total_keys = all_kv.shape[0]
    keys_all = all_kv[:, 0].reshape(total_keys, local_heads, head_dim)
    values_all = all_kv[:, 1].reshape(total_keys, local_heads, head_dim)
    scores = (
        jnp.einsum("qhd,khd->hqk", queries, keys_all, preferred_element_type=jnp.float32) * scale
    )
    masked = all_pos[None, None, :] > kept_pos[None, :, None]
    scores = jnp.where(masked, -jnp.inf, scores)
    top = jnp.max(scores, axis=2, keepdims=True)
    expo = jnp.exp(scores - top)
    numer = jnp.einsum(
        "hqk,khd->hqd", expo.astype(jnp.bfloat16), values_all, preferred_element_type=jnp.float32
    )
    result = numer / jnp.sum(expo, axis=2)[..., None]
    return jnp.transpose(result, (1, 0, 2)).reshape(capacity, columns).astype(jnp.bfloat16)


def solution(mesh):
    in_specs = (P("seq", "tp"), P("seq", None, "tp"), P("seq"), P("seq"))
    out_specs = P("seq", "tp")
    return jax.shard_map(
        on_device, mesh=mesh, in_specs=in_specs, out_specs=out_specs, check_vma=False
    )
```

profile of v0, /device:TPU:0, one launch (start us, length us, event | category | flops | bytes accessed | tf_op | source)
XLA Modules:
  0.0 104.7 jit_solution(6532559039854450984)
XLA Ops:
  6.5 0.7 all-gather.3.cloned.1.call-update
  7.9 1.2 %dynamic-slice = u32[1]{0:T(128)} dynamic-slice(u32[32]{0:T(128)} %constant.83, u32[]{:T(128)S(6)} %add.147), dynamic_slice_sizes={1} | dynamic-slice | bytes 12
  9.1 0.7 dynamic-update-slice
  9.8 8.8 %all-reduce = s32[4]{0:T(128)S(1)} all-reduce(s32[4]{0:T(128)S(1)} %dynamic-update-slice), channel_id=2, replica_groups=mesh['seq'=4,'tp'=8] {'seq'}, use_global_device_ids=true, to_apply=%add | all-reduce | flops 4 | bytes 32
  18.6 3.5 %while.13 = (s32[]{:T(128)}, s32[1]{0:T(128)}, s32[]{:T(128)}, s32[4,1]{0,1:T(1,128)S(1)}, s32[]{:T(128)}) while((s32[]{:T(128)}, s32[1]{0:T(128)}, s32[]{:T(128)}, s32[4,1]{0,1:T(1,128)S(1)}, s32[]{:T(128)}) %tuple.38), condition=%wide.region_1.2_spmd, body=%wide.region_0.1_spmd.sunk | while | flops 5 | bytes 115 | solution.py:18
  18.6 0.6 constant_dynamic-slice_fusion.2
  19.8 0.6 constant_dynamic-slice_fusion.2
  21.0 0.6 constant_dynamic-slice_fusion.2
  22.2 0.1 reshape.223
  22.3 1.6 %gather_fusion = s32[128]{0:T(128)S(1)} fusion(s32[128]{0:T(128)} %param.8, s32[1024]{0:T(1024)S(1)} %pad_clamp_fusion.1), kind=kCustom, calls=%fused_computation | custom fusion | bytes 1536 | tf_op jit(solution)/shard_map/gather | solution.py:40
  23.9 0.1 gather.9
  24.0 0.6 copy.17
  24.6 3.2 %all-to-all-start = ((s32[4,32,2]{1,2,0:T(2,128)}), s32[4,32,2]{1,2,0:T(2,128)S(1)}, u32[]{:S(2)}, u32[]{:S(2)}) async-start(s32[4,32,2]{1,2,0:T(2,128)} %copy.17), calls=%async_computation | async-start | bytes 8192 | tf_op jit(solution)/shard_map/all_to_all | solution.py:47
  27.9 0.1 reshape.231
  28.0 0.8 gather_fusion.1
  28.9 0.7 broadcast_select_fusion
  30.2 2.5 %all-to-all-done = s32[4,32,2]{1,2,0:T(2,128)S(1)} async-done(((s32[4,32,2]{1,2,0:T(2,128)}), s32[4,32,2]{1,2,0:T(2,128)S(1)}, u32[]{:S(2)}, u32[]{:S(2)}) %all-to-all-start) | async-done | bytes 1056 | tf_op jit(solution)/shard_map/all_to_all | solution.py:47
  32.7 3.3 %all-to-all-start.1 = ((bf16[4,32,512]{2,1,0:T(8,128)(2,1)}), bf16[4,32,512]{2,1,0:T(8,128)(2,1)S(1)}, u32[]{:S(2)}, u32[]{:S(2)}) async-start(bf16[4,32,512]{2,1,0:T(8,128)(2,1)} %broadcast_select_fusion), calls=%async_computation.1 | async-start | bytes 262144 | tf_op jit(solution)/shard_map/all_to_all | solution.py:46
  36.0 0.1 reshape.219
  36.1 1.0 scatter_custom_fusion
  37.1 0.2 dynamic-update-slice.1
  37.4 7.8 %all-reduce.1 = s32[256]{0:T(256)S(1)} all-reduce(s32[256]{0:T(256)S(1)} %dynamic-update-slice.1), channel_id=1, replica_groups=mesh['seq'=4,'tp'=8] {'seq'}, use_global_device_ids=true, to_apply=%add.1 | all-reduce | flops 256 | bytes 2048
  45.2 0.1 broadcast_compare_fusion
  45.3 1.1 %scatter_custom_fusion.1 = bf16[64,512]{1,0:T(8,128)(2,1)S(1)} fusion(s32[128]{0:T(128)S(1)} %get-tuple-element.98, bf16[128,512]{1,0:T(8,128)(2,1)S(1)} %bitcast.50, bf16[]{:T(256)} %constant.77.clone.1), kind=kCustom, calls=%fused_computation.22 | custom fusion | bytes 65538 | tf_op jit(solution)/shard_map/scatter | solution.py:53
  46.4 15.2 %all_gather.21 = bf16[64,4096]{1,0:T(8,128)(2,1)S(1)} all-gather(bf16[64,512]{1,0:T(8,128)(2,1)S(1)} %scatter_custom_fusion.1), channel_id=1, replica_groups=mesh['seq'=4,'tp'=8] {'tp'}, dimensions={1}, use_global_device_ids=true | all-gather | bytes 589824 | tf_op jit(solution)/shard_map/all_gather | solution.py:55
  61.6 21.9 %all-gather.3.cloned.1.call-done = bf16[4096,3,256]{2,0,1:T(8,128)(2,1)} async-done(((bf16[1024,3,256]{2,0,1:T(8,128)(2,1)}), bf16[4096,3,256]{2,0,1:T(8,128)(2,1)}) %all-gather.3.cloned.1.call-update) | async-done | bytes 6291472 | tf_op jit(solution)/shard_map/all_gather | solution.py:56
  83.5 4.0 %convolution_convert_fusion = bf16[64,3,256]{2,0,1:T(8,128)(2,1)S(1)} fusion(bf16[4096,3,256]{2,0,1:T(8,128)(2,1)} %all-gather.3.cloned.1.call-done, bf16[64,4096]{1,0:T(8,128)(2,1)S(1)} %all_gather.21), kind=kOutput, calls=%fused_computation.5 | convolution fusion | flops 402702336 | bytes 6914048 | tf_op jit(solution)/shard_map/rd,dgc->rgc/dot_general | solution.py:58
  87.5 9.0 %all_gather.23 = bf16[256,2,256]{2,0,1:T(8,128)(2,1)S(1)} all-gather(bf16[64,2,256]{2,0,1:T(8,128)(2,1)S(1)} %slice.29), channel_id=1, replica_groups=mesh['seq'=4,'tp'=8] {'seq'}, dimensions={0}, use_global_device_ids=true | all-gather | bytes 327680 | tf_op jit(solution)/shard_map/all_gather | solution.py:65
  96.6 0.3 fusion.20
  96.8 0.2 fusion.7
  97.0 0.2 fusion.3
  97.2 0.6 copy.35
  (22 shorter events, 0.3 us)
Async XLA Ops:
  6.5 21.5 %copy-start = (bf16[256,512]{1,0:T(8,128)(2,1)S(1)}, bf16[256,512]{1,0:T(8,128)(2,1)}, u32[]{:S(2)}) copy-start(bf16[256,512]{1,0:T(8,128)(2,1)} %param.6) | copy-start | bytes 786436
  6.5 76.9 %all-gather.3.cloned.1.call-start = ((), (), s32[]{:S(2)}) async-start(), calls=%async_computation.2 | async-start | bytes 7864320 | tf_op jit(solution)/shard_map/all_gather | solution.py:56
  24.6 8.0 %all-to-all-start = ((s32[4,32,2]{1,2,0:T(2,128)}), s32[4,32,2]{1,2,0:T(2,128)S(1)}, u32[]{:S(2)}, u32[]{:S(2)}) async-start(s32[4,32,2]{1,2,0:T(2,128)} %copy.17), calls=%async_computation | async-start | bytes 8192 | tf_op jit(solution)/shard_map/all_to_all | solution.py:47
  32.7 12.6 %all-to-all-start.1 = ((bf16[4,32,512]{2,1,0:T(8,128)(2,1)}), bf16[4,32,512]{2,1,0:T(8,128)(2,1)S(1)}, u32[]{:S(2)}, u32[]{:S(2)}) async-start(bf16[4,32,512]{2,1,0:T(8,128)(2,1)} %broadcast_select_fusion), calls=%async_computation.1 | async-start | bytes 262144 | tf_op jit(solution)/shard_map/all_to_all | solution.py:46
Sparse Core Ops, SparseCore 0:
  9.2 74.2 all-gather.2
where the time goes:
time: 105 us
  blocking collectives  40.9 us (39%)
  waiting for transfers between devices  25 us (24%)
  between operations  14.7 us (14%)
  local copies, waits for them, and re-layouts  10 us (10%)
  starting transfers between devices  6.57 us (6%)
  matrix products  4.44 us (4%)
  loops' own time  1.78 us (2%)
  other arithmetic  1.21 us (1%)
    all_gather x1, waiting for transfers between devices, on_device(): piece = lax.all_gather(w_qkv, 'seq', axis=0, tiled=True)  21.9 us
    unnamed x2, blocking collectives  16.7 us
    all_gather x1, blocking collectives, on_device(): full_rows = lax.all_gather(kept, 'tp', axis=1, tiled=True)  15.2 us
    all_gather x1, blocking collectives, on_device(): lax.all_gather(key_values, 'seq', axis=0, tiled=True)  9.02 us
    dot_general x1, matrix products, on_device(): jnp.einsum('rd,dgc->rgc', part_rows, piece, preferred_element_type=jnp.fl...  3.97 us
    all_to_all x1, starting transfers between devices, on_device(): lax.all_to_all(picked, 'seq', split_axis=0, concat_axis=0, tiled=True)  3.32 us
    all_to_all x1, starting transfers between devices, on_device(): lax.all_to_all(meta, 'seq', split_axis=0, concat_axis=0, tiled=True)  3.25 us
    all_to_all x1, waiting for transfers between devices, on_device(): lax.all_to_all(meta, 'seq', split_axis=0, concat_axis=0, tiled=True)  2.48 us
  transfers between devices with their start and end apart: 3, of which 2 were waited for; matrix products, arithmetic and copies ran while one was open for 10% of the time, Pallas kernels for 0%

commit v1 on v0

--- a/solution.py
+++ b/solution.py
@@ -4,6 +4,11 @@
 from jax.sharding import PartitionSpec as P
 
 HD = 128
+
+
+def perform_stacks_all_here(buf, dim_no):
+    val = jax.lax.all_gather(buf, "tp")
+    return jnp.concatenate(val, axis=dim_no)
 
 
 def entering(value, axis, join, neutral):
@@ -52,7 +57,7 @@
     flat = arrived.reshape(shards * per_peer, arrived.shape[2])
     kept = jnp.zeros((capacity, flat.shape[1]), flat.dtype).at[target].set(flat, mode="drop")
     kept_pos = jnp.zeros((capacity,), jnp.int32).at[target].set(arrived_meta[:, 0], mode="drop")
-    full_rows = lax.all_gather(kept, "tp", axis=1, tiled=True)
+    full_rows = perform_stacks_all_here(kept, 1)
     piece = lax.all_gather(w_qkv, "seq", axis=0, tiled=True)
     part_rows = lax.slice_in_dim(full_rows, 0, piece.shape[0], axis=1)
     projected = jnp.einsum(

time: 105 us -> 105 us (level)
  no operation moved by 1% of the time
where the time goes in v1:
time: 105 us
  blocking collectives  40.9 us (39%)
  waiting for transfers between devices  24.5 us (23%)
  between operations  14.7 us (14%)
  local copies, waits for them, and re-layouts  10.5 us (10%)
  starting transfers between devices  6.57 us (6%)
  matrix products  4.44 us (4%)
  loops' own time  1.78 us (2%)
  other arithmetic  1.21 us (1%)
    all_gather x1, waiting for transfers between devices, on_device(): piece = lax.all_gather(w_qkv, 'seq', axis=0, tiled=True)  21.3 us
    unnamed x2, blocking collectives  16.7 us
    all_gather x1, blocking collectives, perform_stacks_all_here(): val = jax.lax.all_gather(buf, 'tp')  15.2 us
    all_gather x1, blocking collectives, on_device(): lax.all_gather(key_values, 'seq', axis=0, tiled=True)  9.02 us
    dot_general x1, matrix products, on_device(): jnp.einsum('rd,dgc->rgc', part_rows, piece, preferred_element_type=jnp.fl...  3.97 us
    all_to_all x1, starting transfers between devices, on_device(): lax.all_to_all(picked, 'seq', split_axis=0, concat_axis=0, tiled=True)  3.32 us
    all_to_all x1, starting transfers between devices, on_device(): lax.all_to_all(meta, 'seq', split_axis=0, concat_axis=0, tiled=True)  3.25 us
    all_to_all x1, waiting for transfers between devices, on_device(): lax.all_to_all(meta, 'seq', split_axis=0, concat_axis=0, tiled=True)  2.48 us
  transfers between devices with their start and end apart: 3, of which 2 were waited for; matrix products, arithmetic and copies ran while one was open for 10% of the time, Pallas kernels for 0%

profile of v1, /device:TPU:0, one launch (start us, length us, event | category | flops | bytes accessed | tf_op | source)
XLA Modules:
  0.0 104.7 jit_solution(2758272804027856466)
XLA Ops:
  6.5 0.7 all-gather.4.cloned.1.call-update
  7.9 1.2 %dynamic-slice = u32[1]{0:T(128)} dynamic-slice(u32[32]{0:T(128)} %constant.83, u32[]{:T(128)S(6)} %add.147), dynamic_slice_sizes={1} | dynamic-slice | bytes 12
  9.1 0.7 dynamic-update-slice
  9.8 8.8 %all-reduce = s32[4]{0:T(128)S(1)} all-reduce(s32[4]{0:T(128)S(1)} %dynamic-update-slice), channel_id=2, replica_groups=mesh['seq'=4,'tp'=8] {'seq'}, use_global_device_ids=true, to_apply=%add | all-reduce | flops 4 | bytes 32
  18.6 3.5 %while.13 = (s32[]{:T(128)}, s32[1]{0:T(128)}, s32[]{:T(128)}, s32[4,1]{0,1:T(1,128)S(1)}, s32[]{:T(128)}) while((s32[]{:T(128)}, s32[1]{0:T(128)}, s32[]{:T(128)}, s32[4,1]{0,1:T(1,128)S(1)}, s32[]{:T(128)}) %tuple.38), condition=%wide.region_1.2_spmd, body=%wide.region_0.1_spmd.sunk | while | flops 5 | bytes 115 | solution.py:23
  18.6 0.6 constant_dynamic-slice_fusion.2
  19.8 0.6 constant_dynamic-slice_fusion.2
  21.0 0.6 constant_dynamic-slice_fusion.2
  22.2 0.1 reshape.231
  22.3 1.6 %gather_fusion = s32[128]{0:T(128)S(1)} fusion(s32[128]{0:T(128)} %param.8, s32[1024]{0:T(1024)S(1)} %pad_clamp_fusion.1), kind=kCustom, calls=%fused_computation | custom fusion | bytes 1536 | tf_op jit(solution)/shard_map/gather | solution.py:45
  23.9 0.1 gather.9
  24.0 0.6 copy.19
  24.6 3.2 %all-to-all-start = ((s32[4,32,2]{1,2,0:T(2,128)}), s32[4,32,2]{1,2,0:T(2,128)S(1)}, u32[]{:S(2)}, u32[]{:S(2)}) async-start(s32[4,32,2]{1,2,0:T(2,128)} %copy.19), calls=%async_computation | async-start | bytes 8192 | tf_op jit(solution)/shard_map/all_to_all | solution.py:52
  27.9 0.1 reshape.239
  28.0 0.8 gather_fusion.1
  28.9 0.7 broadcast_select_fusion
  30.2 2.5 %all-to-all-done = s32[4,32,2]{1,2,0:T(2,128)S(1)} async-done(((s32[4,32,2]{1,2,0:T(2,128)}), s32[4,32,2]{1,2,0:T(2,128)S(1)}, u32[]{:S(2)}, u32[]{:S(2)}) %all-to-all-start) | async-done | bytes 1056 | tf_op jit(solution)/shard_map/all_to_all | solution.py:52
  32.7 3.3 %all-to-all-start.1 = ((bf16[4,32,512]{2,1,0:T(8,128)(2,1)}), bf16[4,32,512]{2,1,0:T(8,128)(2,1)S(1)}, u32[]{:S(2)}, u32[]{:S(2)}) async-start(bf16[4,32,512]{2,1,0:T(8,128)(2,1)} %broadcast_select_fusion), calls=%async_computation.1 | async-start | bytes 262144 | tf_op jit(solution)/shard_map/all_to_all | solution.py:51
  36.1 1.0 scatter_custom_fusion
  37.1 0.2 dynamic-update-slice.1
  37.4 7.8 %all-reduce.1 = s32[256]{0:T(256)S(1)} all-reduce(s32[256]{0:T(256)S(1)} %dynamic-update-slice.1), channel_id=1, replica_groups=mesh['seq'=4,'tp'=8] {'seq'}, use_global_device_ids=true, to_apply=%add.1 | all-reduce | flops 256 | bytes 2048
  45.3 1.1 %scatter_custom_fusion.1 = bf16[64,512]{1,0:T(8,128)(2,1)S(1)} fusion(s32[128]{0:T(128)S(1)} %get-tuple-element.98, bf16[128,512]{1,0:T(8,128)(2,1)S(1)} %bitcast.52, bf16[]{:T(256)} %constant.77.clone.1), kind=kCustom, calls=%fused_computation.21 | custom fusion | bytes 65538 | tf_op jit(solution)/shard_map/scatter | solution.py:58
  46.4 15.2 %all-gather.1 = bf16[512,512]{1,0:T(8,128)(2,1)S(1)} all-gather(bf16[64,512]{1,0:T(8,128)(2,1)S(1)} %scatter_custom_fusion.1), channel_id=3, replica_groups=mesh['seq'=4,'tp'=8] {'tp'}, dimensions={0}, use_global_device_ids=true | all-gather | bytes 589824 | tf_op jit(solution)/shard_map/all_gather | solution.py:10
  61.6 0.3 copy.21
  61.9 0.2 reshape.276
  62.1 21.3 %all-gather.4.cloned.1.call-done = bf16[4096,3,256]{2,0,1:T(8,128)(2,1)} async-done(((bf16[1024,3,256]{2,0,1:T(8,128)(2,1)}), bf16[4096,3,256]{2,0,1:T(8,128)(2,1)}) %all-gather.4.cloned.1.call-update) | async-done | bytes 6291472 | tf_op jit(solution)/shard_map/all_gather | solution.py:61
  83.5 4.0 %convolution_convert_fusion = bf16[64,3,256]{2,0,1:T(8,128)(2,1)S(1)} fusion(bf16[64,4096,1]{1,0,2:T(8,128)(2,1)S(1)} %reshape.276, bf16[4096,3,256]{2,0,1:T(8,128)(2,1)} %all-gather.4.cloned.1.call-done), kind=kOutput, calls=%fused_computation.5 | convolution fusion | flops 402702336 | bytes 6914048 | tf_op jit(solution)/shard_map/rd,dgc->rgc/dot_general | solution.py:63
  87.5 9.0 %all_gather.27 = bf16[256,2,256]{2,0,1:T(8,128)(2,1)S(1)} all-gather(bf16[64,2,256]{2,0,1:T(8,128)(2,1)S(1)} %slice.29), channel_id=1, replica_groups=mesh['seq'=4,'tp'=8] {'seq'}, dimensions={0}, use_global_device_ids=true | all-gather | bytes 327680 | tf_op jit(solution)/shard_map/all_gather | solution.py:70
  96.6 0.3 fusion.19
  96.8 0.2 fusion.6
  97.0 0.2 fusion.3
  97.2 0.6 copy.38
  (24 shorter events, 0.5 us)
Async XLA Ops:
  6.5 21.5 %copy-start = (bf16[256,512]{1,0:T(8,128)(2,1)S(1)}, bf16[256,512]{1,0:T(8,128)(2,1)}, u32[]{:S(2)}) copy-start(bf16[256,512]{1,0:T(8,128)(2,1)} %param.6) | copy-start | bytes 786436
  6.5 76.9 %all-gather.4.cloned.1.call-start = ((), (), s32[]{:S(2)}) async-start(), calls=%async_computation.2 | async-start | bytes 7864320 | tf_op jit(solution)/shard_map/all_gather | solution.py:61
  24.6 8.0 %all-to-all-start = ((s32[4,32,2]{1,2,0:T(2,128)}), s32[4,32,2]{1,2,0:T(2,128)S(1)}, u32[]{:S(2)}, u32[]{:S(2)}) async-start(s32[4,32,2]{1,2,0:T(2,128)} %copy.19), calls=%async_computation | async-start | bytes 8192 | tf_op jit(solution)/shard_map/all_to_all | solution.py:52
  32.7 12.6 %all-to-all-start.1 = ((bf16[4,32,512]{2,1,0:T(8,128)(2,1)}), bf16[4,32,512]{2,1,0:T(8,128)(2,1)S(1)}, u32[]{:S(2)}, u32[]{:S(2)}) async-start(bf16[4,32,512]{2,1,0:T(8,128)(2,1)} %broadcast_select_fusion), calls=%async_computation.1 | async-start | bytes 262144 | tf_op jit(solution)/shard_map/all_to_all | solution.py:51
Sparse Core Ops, SparseCore 0:
  9.2 74.2 all-gather.3
